TPU v7x, 16 devices: a whole 2x2x2 slice. The times are simulated.
16 devices in a mesh: col: 4 (over z, y), row: 4 (over x, core).
Axes of the slice: x: 2, y: 2, z: 2, core: 2. Of those that a mesh axis runs over, the one named last changes fastest.
Arguments:
- matrix: bfloat16 [12288, 12288], P('row', 'col')
- y_start: float32 [12288, 32], P(('col', 'row'))
- center: float32 [], replicated
- half_width: float32 [], replicated
Outputs:
- output 1: float32 [12288, 32], P(('col', 'row'))
- output 2: float32 [32, 32], replicated
All inputs are finite; a program needn't handle non-finite values.
Results may differ from a plain program's by a relative error of at most 0.012416.
Values are sent between devices in bfloat16 or wider.
A program may use at most 1 GiB of HBM per device.

v0:
```python
import jax
import jax.numpy as jnp
from jax import lax
from jax.sharding import PartitionSpec as P

DEGREE = 8


def solution(mesh):
    row_count = mesh.shape["row"]
    col_count = mesh.shape["col"]
    both_axes = ("col", "row")
    realign_pairs = [(col_idx * row_count + row_idx, row_idx * col_count + col_idx) for row_idx in range(row_count) for col_idx in range(col_count)]

    def apply_matrix(mat_tile, y_low):
        src_block = lax.all_gather(y_low, "row", axis=0, tiled=True)
        part_sum = jnp.dot(mat_tile, src_block, preferred_element_type=jnp.float32)
        folded = lax.psum_scatter(part_sum, "col", scatter_dimension=0, tiled=True)
        return lax.ppermute(folded, both_axes, realign_pairs)

    def local_filter(mat_tile, y_start, center, half_width):
        y_prev = y_start
        y_cur = (apply_matrix(mat_tile, y_start.astype(jnp.bfloat16)) - center * y_start) / half_width
        for step_index in range(DEGREE - 1):
            y_next = 2.0 * (apply_matrix(mat_tile, y_cur.astype(jnp.bfloat16)) - center * y_cur) / half_width - y_prev
            y_prev = y_cur
            y_cur = y_next
        y_low = y_cur.astype(jnp.bfloat16)
        image_low = apply_matrix(mat_tile, y_low).astype(jnp.bfloat16)
        local_gram = jnp.einsum("pa,pb->ab", y_low, image_low, preferred_element_type=jnp.float32)
        gram_mat = lax.psum(local_gram, both_axes) / (mat_tile.shape[0] * row_count)
        return y_cur, gram_mat

    return jax.shard_map(local_filter, mesh=mesh, in_specs=(P("row", "col"), P(both_axes, None), P(), P()), out_specs=(P(both_axes, None), P()), check_vma=False)
```

profile of v0, /device:TPU:0, one launch (start us, length us, event | category | flops | bytes accessed | tf_op | source)
XLA Modules:
  0.0 482.8 jit_solution(14861248813282523829)
XLA Ops:
  8.1 7.1 %all_gather.27 = bf16[3072,32]{0,1:T(8,128)(2,1)S(1)} all-gather(bf16[768,32]{0,1:T(8,128)(2,1)S(1)} %convert_element_type.30), channel_id=1, replica_groups=mesh['col'=4,'row'=4] {'row'}, dimensions={0}, use_global_device_ids=true | all-gather | bytes 245760 | tf_op jit(solution)/shard_map/all_gather | solution.py:16
  15.3 12.7 %fusion.10 = f32[3072,32]{0,1:T(8,128)} fusion(bf16[3072,3072]{1,0:T(8,128)(2,1)} %param.4, bf16[3072,32]{0,1:T(8,128)(2,1)S(1)} %all_gather.27), kind=kOutput, calls=%fused_computation.27 | convolution fusion | flops 603979776 | bytes 19464192 | tf_op jit(solution)/shard_map/dot_general | solution.py:17
  28.1 22.2 %reduce-scatter.10.cloned.1.call-done = f32[768,32]{0,1:T(8,128)} async-done(((f32[3072,32]{0,1:T(8,128)}), f32[768,32]{0,1:T(8,128)}) %reduce-scatter.10.cloned.1.call-update) | async-done | bytes 98320 | tf_op jit(solution)/shard_map/reduce_scatter | solution.py:18
  50.3 1.5 collective-permute-start
  53.2 10.6 %all_gather.28 = bf16[3072,32]{0,1:T(8,128)(2,1)S(1)} all-gather(bf16[768,32]{0,1:T(8,128)(2,1)S(1)} %fusion.3), channel_id=1, replica_groups=mesh['col'=4,'row'=4] {'row'}, dimensions={0}, use_global_device_ids=true | all-gather | bytes 245760 | tf_op jit(solution)/shard_map/all_gather | solution.py:16
  63.8 12.7 %convolution_bitcast_fusion.7 = f32[3072,32]{0,1:T(8,128)} fusion(bf16[3072,32]{0,1:T(8,128)(2,1)S(1)} %all_gather.28, bf16[3072,3072]{1,0:T(8,128)(2,1)} %param.4), kind=kOutput, calls=%fused_computation.7 | convolution fusion | flops 603979776 | bytes 19464192 | tf_op jit(solution)/shard_map/dot_general | solution.py:17
  76.6 21.5 %reduce-scatter.12.cloned.1.call-done = f32[768,32]{0,1:T(8,128)} async-done(((f32[3072,32]{0,1:T(8,128)}), f32[768,32]{0,1:T(8,128)}) %reduce-scatter.12.cloned.1.call-update) | async-done | bytes 98320 | tf_op jit(solution)/shard_map/reduce_scatter | solution.py:18
  98.1 1.5 collective-permute-start.1
  99.7 12.3 %all_gather.29 = bf16[3072,32]{0,1:T(8,128)(2,1)S(1)} all-gather(bf16[768,32]{0,1:T(8,128)(2,1)S(1)} %get-tuple-element.12), channel_id=1, replica_groups=mesh['col'=4,'row'=4] {'row'}, dimensions={0}, use_global_device_ids=true | all-gather | bytes 245760 | tf_op jit(solution)/shard_map/all_gather | solution.py:16
  112.0 12.7 %convolution_bitcast_fusion.6 = f32[3072,32]{0,1:T(8,128)} fusion(bf16[3072,32]{0,1:T(8,128)(2,1)S(1)} %all_gather.29, bf16[3072,3072]{1,0:T(8,128)(2,1)} %param.4), kind=kOutput, calls=%fused_computation.6 | convolution fusion | flops 603979776 | bytes 19464192 | tf_op jit(solution)/shard_map/dot_general | solution.py:17
  124.8 21.5 %reduce-scatter.14.cloned.1.call-done = f32[768,32]{0,1:T(8,128)} async-done(((f32[3072,32]{0,1:T(8,128)}), f32[768,32]{0,1:T(8,128)}) %reduce-scatter.14.cloned.1.call-update) | async-done | bytes 98320 | tf_op jit(solution)/shard_map/reduce_scatter | solution.py:18
  146.3 1.5 collective-permute-start.2
  147.9 12.0 %all_gather.30 = bf16[3072,32]{0,1:T(8,128)(2,1)S(1)} all-gather(bf16[768,32]{0,1:T(8,128)(2,1)S(1)} %get-tuple-element.10), channel_id=1, replica_groups=mesh['col'=4,'row'=4] {'row'}, dimensions={0}, use_global_device_ids=true | all-gather | bytes 245760 | tf_op jit(solution)/shard_map/all_gather | solution.py:16
  159.8 12.7 %convolution_bitcast_fusion.5 = f32[3072,32]{0,1:T(8,128)} fusion(bf16[3072,32]{0,1:T(8,128)(2,1)S(1)} %all_gather.30, bf16[3072,3072]{1,0:T(8,128)(2,1)} %param.4), kind=kOutput, calls=%fused_computation.5 | convolution fusion | flops 603979776 | bytes 19464192 | tf_op jit(solution)/shard_map/dot_general | solution.py:17
  172.7 21.5 %reduce-scatter.16.cloned.1.call-done = f32[768,32]{0,1:T(8,128)} async-done(((f32[3072,32]{0,1:T(8,128)}), f32[768,32]{0,1:T(8,128)}) %reduce-scatter.16.cloned.1.call-update) | async-done | bytes 98320 | tf_op jit(solution)/shard_map/reduce_scatter | solution.py:18
  194.2 1.5 collective-permute-start.3
  195.7 12.4 %all_gather.31 = bf16[3072,32]{0,1:T(8,128)(2,1)S(1)} all-gather(bf16[768,32]{0,1:T(8,128)(2,1)S(1)} %get-tuple-element.8), channel_id=1, replica_groups=mesh['col'=4,'row'=4] {'row'}, dimensions={0}, use_global_device_ids=true | all-gather | bytes 245760 | tf_op jit(solution)/shard_map/all_gather | solution.py:16
  208.2 12.7 %convolution_bitcast_fusion.4 = f32[3072,32]{0,1:T(8,128)} fusion(bf16[3072,32]{0,1:T(8,128)(2,1)S(1)} %all_gather.31, bf16[3072,3072]{1,0:T(8,128)(2,1)} %param.4), kind=kOutput, calls=%fused_computation.4 | convolution fusion | flops 603979776 | bytes 19464192 | tf_op jit(solution)/shard_map/dot_general | solution.py:17
  221.0 21.5 %reduce-scatter.18.cloned.1.call-done = f32[768,32]{0,1:T(8,128)} async-done(((f32[3072,32]{0,1:T(8,128)}), f32[768,32]{0,1:T(8,128)}) %reduce-scatter.18.cloned.1.call-update) | async-done | bytes 98320 | tf_op jit(solution)/shard_map/reduce_scatter | solution.py:18
  244.1 12.0 %all_gather.32 = bf16[3072,32]{0,1:T(8,128)(2,1)S(1)} all-gather(bf16[768,32]{0,1:T(8,128)(2,1)S(1)} %get-tuple-element.6), channel_id=1, replica_groups=mesh['col'=4,'row'=4] {'row'}, dimensions={0}, use_global_device_ids=true | all-gather | bytes 245760 | tf_op jit(solution)/shard_map/all_gather | solution.py:16
  256.0 12.7 %convolution_bitcast_fusion.3 = f32[3072,32]{0,1:T(8,128)} fusion(bf16[3072,32]{0,1:T(8,128)(2,1)S(1)} %all_gather.32, bf16[3072,3072]{1,0:T(8,128)(2,1)} %param.4), kind=kOutput, calls=%fused_computation.3 | convolution fusion | flops 603979776 | bytes 19464192 | tf_op jit(solution)/shard_map/dot_general | solution.py:17
  268.9 21.5 %reduce-scatter.20.cloned.1.call-done = f32[768,32]{0,1:T(8,128)} async-done(((f32[3072,32]{0,1:T(8,128)}), f32[768,32]{0,1:T(8,128)}) %reduce-scatter.20.cloned.1.call-update) | async-done | bytes 98320 | tf_op jit(solution)/shard_map/reduce_scatter | solution.py:18
  291.9 12.1 %all_gather.33 = bf16[3072,32]{0,1:T(8,128)(2,1)S(1)} all-gather(bf16[768,32]{0,1:T(8,128)(2,1)S(1)} %get-tuple-element.4), channel_id=1, replica_groups=mesh['col'=4,'row'=4] {'row'}, dimensions={0}, use_global_device_ids=true | all-gather | bytes 245760 | tf_op jit(solution)/shard_map/all_gather | solution.py:16
  304.1 12.7 %convolution_bitcast_fusion.2 = f32[3072,32]{0,1:T(8,128)} fusion(bf16[3072,32]{0,1:T(8,128)(2,1)S(1)} %all_gather.33, bf16[3072,3072]{1,0:T(8,128)(2,1)} %param.4), kind=kOutput, calls=%fused_computation.2 | convolution fusion | flops 603979776 | bytes 19464192 | tf_op jit(solution)/shard_map/dot_general | solution.py:17
  316.9 21.5 %reduce-scatter.22.cloned.1.call-done = f32[768,32]{0,1:T(8,128)} async-done(((f32[3072,32]{0,1:T(8,128)}), f32[768,32]{0,1:T(8,128)}) %reduce-scatter.22.cloned.1.call-update) | async-done | bytes 98320 | tf_op jit(solution)/shard_map/reduce_scatter | solution.py:18
  339.9 12.0 %all_gather.34 = bf16[3072,32]{0,1:T(8,128)(2,1)S(1)} all-gather(bf16[768,32]{0,1:T(8,128)(2,1)S(1)} %fusion.2), channel_id=1, replica_groups=mesh['col'=4,'row'=4] {'row'}, dimensions={0}, use_global_device_ids=true | all-gather | bytes 245760 | tf_op jit(solution)/shard_map/all_gather | solution.py:16
  351.9 12.7 %convolution_bitcast_fusion.1 = f32[3072,32]{0,1:T(8,128)} fusion(bf16[3072,32]{0,1:T(8,128)(2,1)S(1)} %all_gather.34, bf16[3072,3072]{1,0:T(8,128)(2,1)} %param.4), kind=kOutput, calls=%fused_computation.1 | convolution fusion | flops 603979776 | bytes 19464192 | tf_op jit(solution)/shard_map/dot_general | solution.py:17
  364.7 21.5 %reduce-scatter.24.cloned.1.call-done = f32[768,32]{0,1:T(8,128)} async-done(((f32[3072,32]{0,1:T(8,128)}), f32[768,32]{0,1:T(8,128)}) %reduce-scatter.24.cloned.1.call-update) | async-done | bytes 98320 | tf_op jit(solution)/shard_map/reduce_scatter | solution.py:18
  388.4 12.1 %all_gather.35 = bf16[3072,32]{0,1:T(8,128)(2,1)S(1)} all-gather(bf16[768,32]{0,1:T(8,128)(2,1)S(1)} %get-tuple-element.2), channel_id=1, replica_groups=mesh['col'=4,'row'=4] {'row'}, dimensions={0}, use_global_device_ids=true | all-gather | bytes 245760 | tf_op jit(solution)/shard_map/all_gather | solution.py:16
  400.5 12.7 %convolution_bitcast_fusion = f32[3072,32]{0,1:T(8,128)} fusion(bf16[3072,32]{0,1:T(8,128)(2,1)S(1)} %all_gather.35, bf16[3072,3072]{1,0:T(8,128)(2,1)} %param.4), kind=kOutput, calls=%fused_computation | convolution fusion | flops 603979776 | bytes 19464192 | tf_op jit(solution)/shard_map/dot_general | solution.py:17
  413.3 21.6 %reduce-scatter.26.cloned.1.call-done = f32[768,32]{0,1:T(8,128)} async-done(((f32[3072,32]{0,1:T(8,128)}), f32[768,32]{0,1:T(8,128)}) %reduce-scatter.26.cloned.1.call-update) | async-done | bytes 98320 | tf_op jit(solution)/shard_map/reduce_scatter | solution.py:18
  436.6 38.9 %psum.7 = f32[32,32]{1,0:T(8,128)S(1)} all-reduce(f32[32,32]{1,0:T(8,128)S(1)} %fusion), channel_id=1, replica_groups=mesh['col'=4,'row'=4] {'col','row'}, use_global_device_ids=true, to_apply=%region_9.0 | all-reduce | flops 1024 | bytes 8192 | tf_op jit(solution)/shard_map/psum | solution.py:31
  (45 shorter events, 10.8 us)
Async XLA Ops:
  7.2 46.0 %copy-start = (f32[768,32]{0,1:T(8,128)S(1)}, f32[768,32]{0,1:T(8,128)}, u32[]{:S(2)}) copy-start(f32[768,32]{0,1:T(8,128)} %param.5) | copy-start | bytes 294916
  7.2 43.1 %reduce-scatter.10.cloned.1.call-start = ((), (), s32[]{:S(2)}) async-start(), calls=%async_computation.9 | async-start | bytes 491520 | tf_op jit(solution)/shard_map/reduce_scatter | solution.py:18
  28.0 70.1 %reduce-scatter.12.cloned.1.call-start = ((), (), s32[]{:S(2)}) async-start(), calls=%async_computation.10 | async-start | bytes 491520 | tf_op jit(solution)/shard_map/reduce_scatter | solution.py:18
  50.3 2.8 collective-permute-start
  76.6 69.7 %reduce-scatter.14.cloned.1.call-start = ((), (), s32[]{:S(2)}) async-start(), calls=%async_computation.11 | async-start | bytes 491520 | tf_op jit(solution)/shard_map/reduce_scatter | solution.py:18
  98.1 1.5 collective-permute-start.1
  124.8 69.4 %reduce-scatter.16.cloned.1.call-start = ((), (), s32[]{:S(2)}) async-start(), calls=%async_computation.12 | async-start | bytes 491520 | tf_op jit(solution)/shard_map/reduce_scatter | solution.py:18
  146.3 1.5 collective-permute-start.2
  172.6 69.9 %reduce-scatter.18.cloned.1.call-start = ((), (), s32[]{:S(2)}) async-start(), calls=%async_computation.13 | async-start | bytes 491520 | tf_op jit(solution)/shard_map/reduce_scatter | solution.py:18
  194.2 1.5 collective-permute-start.3
  220.9 69.4 %reduce-scatter.20.cloned.1.call-start = ((), (), s32[]{:S(2)}) async-start(), calls=%async_computation.14 | async-start | bytes 491520 | tf_op jit(solution)/shard_map/reduce_scatter | solution.py:18
  242.5 1.5 collective-permute-start.4
  268.8 69.6 %reduce-scatter.22.cloned.1.call-start = ((), (), s32[]{:S(2)}) async-start(), calls=%async_computation.15 | async-start | bytes 491520 | tf_op jit(solution)/shard_map/reduce_scatter | solution.py:18
  290.4 1.5 collective-permute-start.5
  316.8 69.4 %reduce-scatter.24.cloned.1.call-start = ((), (), s32[]{:S(2)}) async-start(), calls=%async_computation.16 | async-start | bytes 491520 | tf_op jit(solution)/shard_map/reduce_scatter | solution.py:18
  338.4 1.5 collective-permute-start.6
  364.7 70.2 %reduce-scatter.26.cloned.1.call-start = ((), (), s32[]{:S(2)}) async-start(), calls=%async_computation.17 | async-start | bytes 491520 | tf_op jit(solution)/shard_map/reduce_scatter | solution.py:18
  386.2 1.5 collective-permute-start.7
  434.9 1.5 collective-permute-start.8
Sparse Core Ops, SparseCore 0:
  28.1 22.1 reduce-scatter.9
  76.7 21.3 reduce-scatter.11
  124.9 21.3 reduce-scatter.13
  172.7 21.3 reduce-scatter.15
  221.1 21.3 reduce-scatter.17
  268.9 21.3 reduce-scatter.19
  316.9 21.3 reduce-scatter.21
  364.8 21.3 reduce-scatter.23
  413.4 21.4 reduce-scatter.25
where the time goes:
time: 490 us; the launch traced here: 483 us
  waiting for transfers between devices  194 us (40%)
  blocking collectives  141 us (29%)
  matrix products  115 us (23%)
  between operations  15.4 us (3%)
  starting transfers between devices  14.2 us (3%)
    reduce_scatter x9, waiting for transfers between devices, apply_matrix(): folded = lax.psum_scatter(part_sum, 'col', scatter_dimension=0, tiled=True)  194 us
    dot_general x9, matrix products, apply_matrix(): part_sum = jnp.dot(mat_tile, src_block, preferred_element_type=jnp.float32)  115 us
    all_gather x9, blocking collectives, apply_matrix(): src_block = lax.all_gather(y_low, 'row', axis=0, tiled=True)  103 us
    psum x1, blocking collectives, local_filter(): gram_mat = lax.psum(local_gram, both_axes) / (mat_tile.shape[0] * row_count)  38.9 us
    ppermute x9, starting transfers between devices, apply_matrix(): return lax.ppermute(folded, both_axes, realign_pairs)  13.8 us
  transfers between devices with their start and end apart: 18, of which 9 were waited for; matrix products, arithmetic and copies ran while one was open for 0% of the time, Pallas kernels for 0%

commit v1 on v0

v1 whole, which is shorter than its diff:
```python
import functools

import jax
import jax.numpy as jnp
from jax import lax
from jax.experimental import pallas as pl
from jax.experimental.pallas import tpu as pltpu
from jax.sharding import PartitionSpec as P

DEGREE = 8
MESH = pl.DeviceIdType.MESH


def filter_kernel(rows, cols, a_hbm, y_in, c_in, e_in, y_out, g_out, a_v, part, y_cur, y_prev, y_send, y_got, pair_got, x_got, g_send, g_got,
                  a_sem, gat_send, gat_recv, pair_send, pair_recv, x_send, x_recv, g_ssem, g_rsem):
    i = lax.axis_index("row")
    j = lax.axis_index("col")
    width, piece = y_in.shape
    n_all = piece * rows * cols

    def block_copy(kq, nq):
        src_rows = pl.ds(pl.multiple_of((i ^ kq) * piece, piece), piece)
        src_cols = pl.ds(pl.multiple_of((i ^ nq) * piece, piece), piece)
        return pltpu.make_async_copy(a_hbm.at[src_rows, src_cols], a_v.at[nq, kq], a_sem.at[kq, nq])

    order = (3, 2, 1, 0)
    for kq in range(4):
        for nq in order:
            block_copy(kq, nq).start()

    barrier = pltpu.get_barrier_semaphore()
    for dr in range(rows):
        for dc in range(cols):
            if dr or dc:
                pl.semaphore_signal(barrier, inc=1, device_id={"row": i ^ dr, "col": j ^ dc}, device_id_type=MESH)
    pl.semaphore_wait(barrier, rows * cols - 1)

    center = c_in[0, 0]
    half_width = e_in[0, 0]
    y_cur[...] = y_in[...]
    y_prev[...] = jnp.zeros_like(y_prev)
    y_send[...] = y_in[...].astype(jnp.bfloat16)

    def gather_copy(dc, par):
        return pltpu.make_async_remote_copy(
            src_ref=y_send, dst_ref=y_got.at[par, i ^ j], send_sem=gat_send.at[dc], recv_sem=gat_recv.at[par, i ^ j],
            device_id={"row": j, "col": j ^ dc}, device_id_type=MESH)

    def gather_arrival(kq, par):
        return pltpu.make_async_remote_copy(
            src_ref=y_send, dst_ref=y_got.at[par, kq], send_sem=gat_send.at[0], recv_sem=gat_recv.at[par, kq],
            device_id={"row": j, "col": j ^ 1}, device_id_type=MESH)

    def pair_copy(q, par):
        return pltpu.make_async_remote_copy(
            src_ref=part.at[2 * q + 1], dst_ref=pair_got.at[par, q], send_sem=pair_send.at[q], recv_sem=pair_recv.at[par, q],
            device_id={"row": i ^ 1, "col": j}, device_id_type=MESH)

    def x_copy(par):
        return pltpu.make_async_remote_copy(
            src_ref=part.at[2], dst_ref=x_got.at[par], send_sem=x_send, recv_sem=x_recv.at[par],
            device_id={"row": i ^ 2, "col": j}, device_id_type=MESH)

    def apply(t, first):
        par = lax.rem(t, 2)

        @pl.when(i != j)
        def _():
            gather_copy(0, par).start()

        @pl.when(i == j)
        def _():
            y_got[par, 0] = y_send[...]

        for dc in (3, 2, 1):
            gather_copy(dc, par).start()

        for kq in range(4):
            if kq == 0:
                @pl.when(i != j)
                def _():
                    gather_arrival(0, par).wait_recv()
            else:
                gather_arrival(kq, par).wait_recv()
            for nq in order:
                if first:
                    block_copy(kq, nq).wait()
                prod = jnp.dot(y_got[par, kq], a_v[nq, kq], preferred_element_type=jnp.float32)
                part[nq] = prod if kq == 0 else part[nq] + prod
                if kq == 3 and nq % 2 == 1:
                    pair_copy(nq // 2, par).start()

        pair_copy(1, par).wait_recv()
        part[2] = part[2] + pair_got[par, 1]
        x_copy(par).start()
        pair_copy(0, par).wait_recv()
        own = part[0] + pair_got[par, 0]
        x_copy(par).wait_recv()
        image = own + x_got[par]

        @pl.when(i != j)
        def _():
            gather_copy(0, par).wait_send()

        for dc in (3, 2, 1):
            gather_copy(dc, par).wait_send()
        pair_copy(1, par).wait_send()
        pair_copy(0, par).wait_send()
        x_copy(par).wait_send()
        return image

    def advance(t, factor, image):
        y_next = factor * (image - center * y_cur[...]) / half_width - y_prev[...]
        y_prev[...] = y_cur[...]
        y_cur[...] = y_next
        y_send[...] = y_next.astype(jnp.bfloat16)

    advance(0, 1.0, apply(0, True))

    def step(t, carry):
        advance(t, 2.0, apply(t, False))
        return carry

    lax.fori_loop(1, DEGREE, step, 0)
    y_out[...] = y_cur[...]
    image_low = apply(DEGREE, False).astype(jnp.bfloat16)
    gram = lax.dot_general(y_send[...], image_low, (((1,), (1,)), ((), ())), preferred_element_type=jnp.float32)
    strip = width // 4
    g_send[...] = jnp.concatenate([gram[strip * s: strip * (s + 1)] for s in range(4)], axis=1)
    me = i * cols + j

    def gram_copy(dr, dc):
        idx = dr * cols + dc
        return pltpu.make_async_remote_copy(
            src_ref=g_send, dst_ref=g_got.at[me], send_sem=g_ssem.at[idx], recv_sem=g_rsem.at[me],
            device_id={"row": i ^ dr, "col": j ^ dc}, device_id_type=MESH)

    def gram_arrival(dr, dc):
        src = (i ^ dr) * cols + (j ^ dc)
        return pltpu.make_async_remote_copy(
            src_ref=g_send, dst_ref=g_got.at[src], send_sem=g_ssem.at[0], recv_sem=g_rsem.at[src],
            device_id={"row": i ^ dr, "col": j ^ dc}, device_id_type=MESH)

    pairs = [(dr, dc) for dr in range(rows) for dc in range(cols) if dr or dc]
    for dr, dc in reversed(pairs):
        gram_copy(dr, dc).start()
    g_got[me] = g_send[...]
    for dr, dc in pairs:
        gram_arrival(dr, dc).wait_recv()
    total = g_got[0]
    for k in range(1, rows * cols):
        total = total + g_got[k]
    total = total / n_all
    for s in range(4):
        g_out[strip * s: strip * (s + 1), :] = total[:, width * s: width * (s + 1)]
    for dr, dc in pairs:
        gram_copy(dr, dc).wait_send()


def solution(mesh):
    rows = mesh.shape["row"]
    cols = mesh.shape["col"]
    both_axes = ("col", "row")

    def local_filter(mat_tile, y_start, center, half_width):
        piece, width = y_start.shape
        f32, bf16 = jnp.float32, jnp.bfloat16
        dma = pltpu.SemaphoreType.DMA
        strip = width // 4
        y_t, gram = pl.pallas_call(
            functools.partial(filter_kernel, rows, cols),
            out_shape=(jax.ShapeDtypeStruct((width, piece), f32), jax.ShapeDtypeStruct((width, width), f32)),
            in_specs=[pl.BlockSpec(memory_space=pltpu.HBM), pl.BlockSpec(memory_space=pltpu.VMEM),
                      pl.BlockSpec(memory_space=pltpu.SMEM), pl.BlockSpec(memory_space=pltpu.SMEM)],
            out_specs=(pl.BlockSpec(memory_space=pltpu.VMEM), pl.BlockSpec(memory_space=pltpu.VMEM)),
            scratch_shapes=[
                pltpu.VMEM((4, 4, piece, piece), bf16),
                pltpu.VMEM((4, width, piece), f32),
                pltpu.VMEM((width, piece), f32),
                pltpu.VMEM((width, piece), f32),
                pltpu.VMEM((width, piece), bf16),
                pltpu.VMEM((2, 4, width, piece), bf16),
                pltpu.VMEM((2, 2, width, piece), f32),
                pltpu.VMEM((2, width, piece), f32),
                pltpu.VMEM((strip, 4 * width), f32),
                pltpu.VMEM((rows * cols, strip, 4 * width), f32),
                dma((4, 4)), dma((4,)), dma((2, 4)), dma((2,)), dma((2, 2)), dma, dma((2,)),
                dma((rows * cols,)), dma((rows * cols,)),
            ],
            compiler_params=pltpu.CompilerParams(collective_id=0, has_side_effects=True, vmem_limit_bytes=56 * 1024 * 1024),
        )(mat_tile, y_start.T, center.reshape(1, 1), half_width.reshape(1, 1))
        return y_t.T, gram

    return jax.shard_map(local_filter, mesh=mesh, in_specs=(P("row", "col"), P(both_axes, None), P(), P()),
                         out_specs=(P(both_axes, None), P()), check_vma=False)
```

time: 490 us -> 140 us (0.29); the launches traced: 483 us -> 140 us
  waiting for transfers between devices: 194 us -> 0 us
  blocking collectives: 141 us -> 0 us
  Pallas kernels: 0 us -> 135 us
  matrix products: 115 us -> 0 us
  starting transfers between devices: 14.2 us -> 0 us
  between operations: 15.4 us -> 1.93 us
    reduce_scatter x9 -> x0, waiting for transfers between devices: 194 us -> none  [apply_matrix(): folded = lax.psum_scatter(part_sum, 'col', scatter_dimension=0, tiled=True)]
    pallas_call x0 -> x1, Pallas kernels: none -> 135 us  [local_filter(): pl.pallas_call(functools.partial(filter_kernel, rows, cols), out_shape=(j...]
    dot_general x10 -> x0, matrix products: 115 us -> none  [the longest x9 115 us: apply_matrix(): part_sum = jnp.dot(mat_tile, src_block, preferred_element_type=jnp.float32)]
    all_gather x9 -> x0, blocking collectives: 103 us -> none  [apply_matrix(): src_block = lax.all_gather(y_low, 'row', axis=0, tiled=True)]
    psum x1 -> x0, blocking collectives: 38.9 us -> none  [local_filter(): gram_mat = lax.psum(local_gram, both_axes) / (mat_tile.shape[0] * row_count)]
    ppermute x9 -> x0, starting transfers between devices: 13.8 us -> none  [apply_matrix(): return lax.ppermute(folded, both_axes, realign_pairs)]
  transfers between devices with their start and end apart: 18 -> 0, of which waited for: 9 -> 0; matrix products, arithmetic and copies ran while one was open for 0% -> 0% of each run, Pallas kernels for 0% -> 0%
where the time goes in v1:
time: 140 us
  Pallas kernels  135 us (96%)
  local copies, waits for them, and re-layouts  2.86 us (2%)
  between operations  1.93 us (1%)
    pallas_call x1, Pallas kernels, local_filter(): pl.pallas_call(functools.partial(filter_kernel, rows, cols), out_shape=(j...  135 us
    unnamed x2, local copies, waits for them, and re-layouts  2.86 us

profile of v1, /device:TPU:0, one launch (start us, length us, event | category | flops | bytes accessed | tf_op | source)
XLA Modules:
  0.0 139.6 jit_solution(18347690863277668155)
XLA Ops:
  1.9 134.8 %shard_map.59 = (f32[32,768]{1,0:T(8,128)}, f32[32,32]{1,0:T(8,128)}) custom-call(bf16[3072,3072]{1,0:T(8,128)(2,1)} %a_hbm.1, f32[32,768]{1,0:T(8,128)} %bitcast.6, f32[1,1]{1,0:T(1,128)} %bitcast.4.c_in, f32[1,1]{1,0:T(1,128)} %bitcast.5.e_in), custom_call_target="tpu_custom_call" | custom-call | tf_op jit(solution)/shard_map/pallas_call | solution.py:170
  136.7 1.5 %copy.10 = f32[768,32]{0,1:T(8,128)} copy(f32[768,32]{0,1:T(8,128)} %bitcast.7) | data formatting | bytes 196608
  138.3 1.3 copy.11

commit v2 on v1

v2 whole, which is shorter than its diff:
```python
import functools

import jax
import jax.numpy as jnp
from jax import lax
from jax.experimental import pallas as pl
from jax.experimental.pallas import tpu as pltpu
from jax.sharding import PartitionSpec as P

DEGREE = 8
CHUNK = 256
MESH = pl.DeviceIdType.MESH


def filter_kernel(rows, cols, a_hbm, y_in, c_in, e_in, y_out, g_out, a_v, part, y_cur, y_prev, y_send, y_got, pair_got, x_got, g_send, g_got,
                  a_sem, gat_send, gat_recv, pair_send, pair_recv, x_send, x_recv, g_ssem, g_rsem):
    i = lax.axis_index("row")
    j = lax.axis_index("col")
    width, piece = y_in.shape
    n_all = piece * rows * cols
    chunks = piece // CHUNK
    slots = (3, 1, 2, 0)

    def block_copy(h, n, kq):
        src_rows = pl.ds(pl.multiple_of((i ^ kq) * piece + h * CHUNK, CHUNK), CHUNK)
        src_cols = pl.ds(pl.multiple_of((i ^ slots[n]) * piece, piece), piece)
        return pltpu.make_async_copy(a_hbm.at[src_rows, src_cols], a_v.at[h, n, pl.ds(kq * CHUNK, CHUNK)], a_sem.at[h, n])

    for h in range(chunks):
        for n in range(4):
            for kq in range(4):
                block_copy(h, n, kq).start()

    def block_wait(h, n):
        pltpu.make_async_copy(a_hbm.at[pl.ds(0, 4 * CHUNK), pl.ds(0, piece)], a_v.at[h, n], a_sem.at[h, n]).wait()

    barrier = pltpu.get_barrier_semaphore()
    for dr in range(rows):
        for dc in range(cols):
            if dr or dc:
                pl.semaphore_signal(barrier, inc=1, device_id={"row": i ^ dr, "col": j ^ dc}, device_id_type=MESH)
    pl.semaphore_wait(barrier, rows * cols - 1)

    center = c_in[0, 0]
    half_width = e_in[0, 0]

    def gather_copy(dc, g, par):
        return pltpu.make_async_remote_copy(
            src_ref=y_send.at[g], dst_ref=y_got.at[par, g, i ^ j], send_sem=gat_send.at[g, dc], recv_sem=gat_recv.at[par, g, i ^ j],
            device_id={"row": j, "col": j ^ dc}, device_id_type=MESH)

    def gather_arrival(kq, g, par):
        return pltpu.make_async_remote_copy(
            src_ref=y_send.at[g], dst_ref=y_got.at[par, g, kq], send_sem=gat_send.at[g, 0], recv_sem=gat_recv.at[par, g, kq],
            device_id={"row": j, "col": j ^ 1}, device_id_type=MESH)

    def pair_copy(g, par):
        return pltpu.make_async_remote_copy(
            src_ref=part.at[g, pl.ds(0, 2)], dst_ref=pair_got.at[par, g], send_sem=pair_send.at[g], recv_sem=pair_recv.at[par, g],
            device_id={"row": i ^ 1, "col": j}, device_id_type=MESH)

    def x_copy(g, par):
        return pltpu.make_async_remote_copy(
            src_ref=part.at[g, 2], dst_ref=x_got.at[par, g], send_sem=x_send.at[g], recv_sem=x_recv.at[par, g],
            device_id={"row": i ^ 2, "col": j}, device_id_type=MESH)

    def gather_start(g, par):
        @pl.when(i != j)
        def _():
            gather_copy(0, g, par).start()

        @pl.when(i == j)
        def _():
            y_got[par, g, 0] = y_send[g]

        for dc in (3, 2, 1):
            gather_copy(dc, g, par).start()

    def gather_sent(g, par):
        @pl.when(i != j)
        def _():
            gather_copy(0, g, par).wait_send()

        for dc in (3, 2, 1):
            gather_copy(dc, g, par).wait_send()

    def source(h, par):
        @pl.when(i != j)
        def _():
            gather_arrival(0, h, par).wait_recv()

        for kq in (1, 2, 3):
            gather_arrival(kq, h, par).wait_recv()
        return jnp.concatenate([y_got[par, h, kq] for kq in range(4)], axis=1)

    def apply(par, first, consume):
        for h in range(chunks):
            lhs = source(h, par)
            if first:
                for n in range(4):
                    block_wait(h, n)
            for g in range(chunks):
                for n in range(4):
                    prod = jnp.dot(lhs, a_v[h, n, :, CHUNK * g: CHUNK * (g + 1)], preferred_element_type=jnp.float32)
                    part[g, n] = prod if h == 0 else part[g, n] + prod
                if h == chunks - 1:
                    pair_copy(g, par).start()
        for g in range(chunks):
            pair_copy(g, par).wait_recv()
            part[g, 2] = part[g, 2] + pair_got[par, g, 0]
            x_copy(g, par).start()
        for g in range(chunks):
            own = part[g, 3] + pair_got[par, g, 1]
            x_copy(g, par).wait_recv()
            consume(g, own + x_got[par, g])
        for g in range(chunks):
            pair_copy(g, par).wait_send()
            x_copy(g, par).wait_send()

    def advance(par, factor):
        def consume(g, image):
            y_now = y_cur[g]
            y_next = factor * (image - center * y_now) / half_width - y_prev[g]
            y_prev[g] = y_now
            y_cur[g] = y_next
            gather_sent(g, par)
            y_send[g] = y_next.astype(jnp.bfloat16)
            gather_start(g, 1 - par)
        return consume

    for g in range(chunks):
        y_now = y_in[:, CHUNK * g: CHUNK * (g + 1)]
        y_cur[g] = y_now
        y_prev[g] = jnp.zeros_like(y_now)
        y_send[g] = y_now.astype(jnp.bfloat16)
        gather_start(g, 0)
    apply(0, True, advance(0, 1.0))

    def step(t, carry):
        par = lax.rem(t, 2)
        apply(par, False, advance(par, 2.0))
        return carry

    lax.fori_loop(1, DEGREE, step, 0)
    for g in range(chunks):
        y_out[:, CHUNK * g: CHUNK * (g + 1)] = y_cur[g]
    images = []
    apply(DEGREE % 2, False, lambda g, image: images.append(image.astype(jnp.bfloat16)))
    for g in range(chunks):
        gather_sent(g, DEGREE % 2)
    image_low = jnp.concatenate(images, axis=1)
    y_low = jnp.concatenate([y_send[g] for g in range(chunks)], axis=1)
    gram = lax.dot_general(y_low, image_low, (((1,), (1,)), ((), ())), preferred_element_type=jnp.float32)
    strip = width // 4
    g_send[...] = jnp.concatenate([gram[strip * s: strip * (s + 1)] for s in range(4)], axis=1)
    me = i * cols + j

    def gram_copy(dr, dc):
        idx = dr * cols + dc
        return pltpu.make_async_remote_copy(
            src_ref=g_send, dst_ref=g_got.at[me], send_sem=g_ssem.at[idx], recv_sem=g_rsem.at[me],
            device_id={"row": i ^ dr, "col": j ^ dc}, device_id_type=MESH)

    def gram_arrival(dr, dc):
        src = (i ^ dr) * cols + (j ^ dc)
        return pltpu.make_async_remote_copy(
            src_ref=g_send, dst_ref=g_got.at[src], send_sem=g_ssem.at[0], recv_sem=g_rsem.at[src],
            device_id={"row": i ^ dr, "col": j ^ dc}, device_id_type=MESH)

    pairs = [(dr, dc) for dr in range(rows) for dc in range(cols) if dr or dc]
    for dr, dc in reversed(pairs):
        gram_copy(dr, dc).start()
    g_got[me] = g_send[...]
    for dr, dc in pairs:
        gram_arrival(dr, dc).wait_recv()
    total = g_got[0]
    for k in range(1, rows * cols):
        total = total + g_got[k]
    total = total / n_all
    for s in range(4):
        g_out[strip * s: strip * (s + 1), :] = total[:, width * s: width * (s + 1)]
    for dr, dc in pairs:
        gram_copy(dr, dc).wait_send()


def solution(mesh):
    rows = mesh.shape["row"]
    cols = mesh.shape["col"]
    both_axes = ("col", "row")

    def local_filter(mat_tile, y_start, center, half_width):
        piece, width = y_start.shape
        f32, bf16 = jnp.float32, jnp.bfloat16
        dma = pltpu.SemaphoreType.DMA
        strip = width // 4
        chunks = piece // CHUNK
        y_t, gram = pl.pallas_call(
            functools.partial(filter_kernel, rows, cols),
            out_shape=(jax.ShapeDtypeStruct((width, piece), f32), jax.ShapeDtypeStruct((width, width), f32)),
            in_specs=[pl.BlockSpec(memory_space=pltpu.HBM), pl.BlockSpec(memory_space=pltpu.VMEM),
                      pl.BlockSpec(memory_space=pltpu.SMEM), pl.BlockSpec(memory_space=pltpu.SMEM)],
            out_specs=(pl.BlockSpec(memory_space=pltpu.VMEM), pl.BlockSpec(memory_space=pltpu.VMEM)),
            scratch_shapes=[
                pltpu.VMEM((chunks, 4, 4 * CHUNK, piece), bf16),
                pltpu.VMEM((chunks, 4, width, CHUNK), f32),
                pltpu.VMEM((chunks, width, CHUNK), f32),
                pltpu.VMEM((chunks, width, CHUNK), f32),
                pltpu.VMEM((chunks, width, CHUNK), bf16),
                pltpu.VMEM((2, chunks, 4, width, CHUNK), bf16),
                pltpu.VMEM((2, chunks, 2, width, CHUNK), f32),
                pltpu.VMEM((2, chunks, width, CHUNK), f32),
                pltpu.VMEM((strip, 4 * width), f32),
                pltpu.VMEM((rows * cols, strip, 4 * width), f32),
                dma((chunks, 4)), dma((chunks, 4)), dma((2, chunks, 4)), dma((chunks,)), dma((2, chunks)), dma((chunks,)), dma((2, chunks)),
                dma((rows * cols,)), dma((rows * cols,)),
            ],
            compiler_params=pltpu.CompilerParams(collective_id=0, has_side_effects=True, vmem_limit_bytes=56 * 1024 * 1024),
        )(mat_tile, y_start.T, center.reshape(1, 1), half_width.reshape(1, 1))
        return y_t.T, gram

    return jax.shard_map(local_filter, mesh=mesh, in_specs=(P("row", "col"), P(both_axes, None), P(), P()),
                         out_specs=(P(both_axes, None), P()), check_vma=False)
```

time: 140 us -> 118 us (0.84)
  Pallas kernels: 135 us -> 112 us
    pallas_call x1, Pallas kernels: 135 us -> 112 us  [local_filter(): pl.pallas_call(functools.partial(filter_kernel, rows, cols), out_shape=(j...]
where the time goes in v2:
time: 118 us; the launch traced here: 117 us
  Pallas kernels  112 us (95%)
  local copies, waits for them, and re-layouts  2.86 us (2%)
  between operations  1.93 us (2%)
    pallas_call x1, Pallas kernels, local_filter(): pl.pallas_call(functools.partial(filter_kernel, rows, cols), out_shape=(j...  112 us
    unnamed x2, local copies, waits for them, and re-layouts  2.86 us

profile of v2, /device:TPU:0, one launch (start us, length us, event | category | flops | bytes accessed | tf_op | source)
XLA Modules:
  0.0 117.3 jit_solution(13915590600970870684)
XLA Ops:
  1.9 112.5 %shard_map.59 = (f32[32,768]{1,0:T(8,128)}, f32[32,32]{1,0:T(8,128)}) custom-call(bf16[3072,3072]{1,0:T(8,128)(2,1)} %a_hbm.1, f32[32,768]{1,0:T(8,128)} %bitcast.6, f32[1,1]{1,0:T(1,128)} %bitcast.4.c_in, f32[1,1]{1,0:T(1,128)} %bitcast.5.e_in), custom_call_target="tpu_custom_call" | custom-call | tf_op jit(solution)/shard_map/pallas_call | solution.py:197
  114.4 1.5 %copy.10 = f32[768,32]{0,1:T(8,128)} copy(f32[768,32]{0,1:T(8,128)} %bitcast.7) | data formatting | bytes 196608
  116.0 1.3 %copy.11 = f32[32,32]{1,0:T(8,128)} copy(f32[32,32]{1,0:T(8,128)} %get-tuple-element.9) | data formatting | bytes 8192

commit v3 on v2

--- a/solution.py
+++ b/solution.py
@@ -8,7 +8,7 @@
 from jax.sharding import PartitionSpec as P
 
 DEGREE = 8
-CHUNK = 256
+CHUNK = 128
 MESH = pl.DeviceIdType.MESH
 
 
@@ -19,7 +19,7 @@
     width, piece = y_in.shape
     n_all = piece * rows * cols
     chunks = piece // CHUNK
-    slots = (3, 1, 2, 0)
+    slots = (2, 1, 3, 0)
 
     def block_copy(h, n, kq):
         src_rows = pl.ds(pl.multiple_of((i ^ kq) * piece + h * CHUNK, CHUNK), CHUNK)
@@ -46,13 +46,8 @@
 
     def gather_copy(dc, g, par):
         return pltpu.make_async_remote_copy(
-            src_ref=y_send.at[g], dst_ref=y_got.at[par, g, i ^ j], send_sem=gat_send.at[g, dc], recv_sem=gat_recv.at[par, g, i ^ j],
+            src_ref=y_send.at[g], dst_ref=y_got.at[par, g, i ^ j], send_sem=gat_send.at[g], recv_sem=gat_recv.at[par, g],
             device_id={"row": j, "col": j ^ dc}, device_id_type=MESH)
-
-    def gather_arrival(kq, g, par):
-        return pltpu.make_async_remote_copy(
-            src_ref=y_send.at[g], dst_ref=y_got.at[par, g, kq], send_sem=gat_send.at[g, 0], recv_sem=gat_recv.at[par, g, kq],
-            device_id={"row": j, "col": j ^ 1}, device_id_type=MESH)
 
     def pair_copy(g, par):
         return pltpu.make_async_remote_copy(
@@ -62,35 +57,44 @@
     def x_copy(g, par):
         return pltpu.make_async_remote_copy(
             src_ref=part.at[g, 2], dst_ref=x_got.at[par, g], send_sem=x_send.at[g], recv_sem=x_recv.at[par, g],
-            device_id={"row": i ^ 2, "col": j}, device_id_type=MESH)
+            device_id={"row": i ^ 3, "col": j}, device_id_type=MESH)
 
     def gather_start(g, par):
-        @pl.when(i != j)
-        def _():
-            gather_copy(0, g, par).start()
-
-        @pl.when(i == j)
-        def _():
-            y_got[par, g, 0] = y_send[g]
-
         for dc in (3, 2, 1):
             gather_copy(dc, g, par).start()
 
+        @pl.when(i != j)
+        def _():
+            gather_copy(0, g, par).start()
+
+        @pl.when(i == j)
+        def _():
+            y_got[par, g, 0] = y_send[g]
+
+    def four_blocks(g, par, count):
+        ref = y_got.at[par, g, pl.ds(0, count)]
+        return pltpu.make_async_remote_copy(
+            src_ref=ref, dst_ref=ref, send_sem=gat_send.at[g], recv_sem=gat_recv.at[par, g],
+            device_id={"row": i, "col": j ^ 1}, device_id_type=MESH)
+
     def gather_sent(g, par):
         @pl.when(i != j)
         def _():
-            gather_copy(0, g, par).wait_send()
-
-        for dc in (3, 2, 1):
-            gather_copy(dc, g, par).wait_send()
+            four_blocks(g, par, 4).wait_send()
+
+        @pl.when(i == j)
+        def _():
+            four_blocks(g, par, 3).wait_send()
 
     def source(h, par):
         @pl.when(i != j)
         def _():
-            gather_arrival(0, h, par).wait_recv()
-
-        for kq in (1, 2, 3):
-            gather_arrival(kq, h, par).wait_recv()
+            four_blocks(h, par, 4).wait_recv()
+
+        @pl.when(i == j)
+        def _():
+            four_blocks(h, par, 3).wait_recv()
+
         return jnp.concatenate([y_got[par, h, kq] for kq in range(4)], axis=1)
 
     def apply(par, first, consume):
@@ -100,9 +104,11 @@
                 for n in range(4):
                     block_wait(h, n)
             for g in range(chunks):
+                tile = jnp.concatenate([a_v[h, n, :, CHUNK * g: CHUNK * (g + 1)] for n in range(4)], axis=1)
+                prod = jnp.dot(lhs, tile, preferred_element_type=jnp.float32)
                 for n in range(4):
-                    prod = jnp.dot(lhs, a_v[h, n, :, CHUNK * g: CHUNK * (g + 1)], preferred_element_type=jnp.float32)
-                    part[g, n] = prod if h == 0 else part[g, n] + prod
+                    term = prod[:, CHUNK * n: CHUNK * (n + 1)]
+                    part[g, n] = term if h == 0 else part[g, n] + term
                 if h == chunks - 1:
                     pair_copy(g, par).start()
         for g in range(chunks):
@@ -211,7 +217,7 @@
                 pltpu.VMEM((2, chunks, width, CHUNK), f32),
                 pltpu.VMEM((strip, 4 * width), f32),
                 pltpu.VMEM((rows * cols, strip, 4 * width), f32),
-                dma((chunks, 4)), dma((chunks, 4)), dma((2, chunks, 4)), dma((chunks,)), dma((2, chunks)), dma((chunks,)), dma((2, chunks)),
+                dma((chunks, 4)), dma((chunks,)), dma((2, chunks)), dma((chunks,)), dma((2, chunks)), dma((chunks,)), dma((2, chunks)),
                 dma((rows * cols,)), dma((rows * cols,)),
             ],
             compiler_params=pltpu.CompilerParams(collective_id=0, has_side_effects=True, vmem_limit_bytes=56 * 1024 * 1024),

time: 118 us -> 112 us (0.949)
  Pallas kernels: 112 us -> 107 us
    pallas_call x1, Pallas kernels: 112 us -> 107 us  [local_filter(): pl.pallas_call(functools.partial(filter_kernel, rows, cols), out_shape=(j...]
where the time goes in v3:
time: 112 us; the launch traced here: 111 us
  Pallas kernels  107 us (96%)
  local copies, waits for them, and re-layouts  2.86 us (3%)
  between operations  1.93 us (2%)
    pallas_call x1, Pallas kernels, local_filter(): pl.pallas_call(functools.partial(filter_kernel, rows, cols), out_shape=(j...  107 us
    unnamed x2, local copies, waits for them, and re-layouts  2.86 us

profile of v3, /device:TPU:0, one launch (start us, length us, event | category | flops | bytes accessed | tf_op | source)
XLA Modules:
  0.0 111.3 jit_solution(11162273243787952030)
XLA Ops:
  1.9 106.5 %shard_map.59 = (f32[32,768]{1,0:T(8,128)}, f32[32,32]{1,0:T(8,128)}) custom-call(bf16[3072,3072]{1,0:T(8,128)(2,1)} %a_hbm.1, f32[32,768]{1,0:T(8,128)} %bitcast.6, f32[1,1]{1,0:T(1,128)} %bitcast.4.c_in, f32[1,1]{1,0:T(1,128)} %bitcast.5.e_in), custom_call_target="tpu_custom_call" | custom-call | tf_op jit(solution)/shard_map/pallas_call | solution.py:203
  108.4 1.5 %copy.10 = f32[768,32]{0,1:T(8,128)} copy(f32[768,32]{0,1:T(8,128)} %bitcast.7) | data formatting | bytes 196608
  110.0 1.3 %copy.11 = f32[32,32]{1,0:T(8,128)} copy(f32[32,32]{1,0:T(8,128)} %get-tuple-element.9) | data formatting | bytes 8192
